TPU v7x, 32 devices: a whole 2x2x4 slice. The times are simulated.
32 devices in a mesh: grp: 2 (over y), seg: 4 (over z), tile: 2 (over x), band: 2 (over core).
Axes of the slice: x: 2, y: 2, z: 4, core: 2. Of those that a mesh axis runs over, the one named last changes fastest.
Arguments:
- fields: float32 [6, 4, 128, 512], P(None, ('grp', 'tile'), None, 'seg'), parts along dimension 1, may hold values from 0 to 2400, as said below
- spectral_table: bfloat16 [128, 512], P(None, 'band'), may hold values from 0 to 0.0390625, as said below
- background: float32 [4, 128, 512], P(('grp', 'tile'), None, 'band'), parts along dimension 0, may hold values from 0.2 to 1
- active: int32 [4, 128], P(('grp', 'tile')), parts along dimension 0, may hold values 0 or 1
Outputs:
- radiance: float32 [4, 4, 128, 512], P('seg', ('grp', 'tile'), None, 'band'), parts along dimension 1
- band_mean: float32 [4, 4, 128], P('seg', ('grp', 'tile')), parts along dimension 1
There are 2 independent parts, one for each index of `grp`. A program takes and returns all parts, laid end to end along the dimension named above; an argument that names none is the same for every part. Nothing has to cross between parts.
Inputs may be any that keep to these rules, and one draw needn't show every extreme that they name: fields[0] is a temperature in kelvin between 300 and 2400; fields[1:5] lie between 0.05 and 1; fields[5] lies between 0 and 0.7. `spectral_table`: every entry is positive.
All inputs are finite; a program needn't handle non-finite values. No bound on the sum of `active` on one device may be relied on, other than what follows from the above.
Results may differ from a plain program's by a relative error of at most 0.0003.
Values sent between devices are 32-bit elements; how exact they have to be, the bound alone decides.
A program may use at most 64 MiB of HBM per device.

v0:
```python
import functools
import math

import jax
import jax.numpy as jnp
from jax import lax
from jax.experimental import pallas as pl
from jax.experimental.pallas import tpu as pltpu
from jax.sharding import PartitionSpec as P

NB = 32
NS = 4
NF = NS * NB
EXTRA = 16
C2 = 1.4388
LOG2E = math.log2(math.e)
SUB = 8
BLOCK = 64
PAIRS = 4
MESH = pl.DeviceIdType.MESH


def prepare(fields_ref, table_ref, active_ref, table_t, weights, inv_t, ratio, ft, step_w):
    pixels = fields_ref.shape[1]
    cells = fields_ref.shape[2]
    table_t[:, :NF] = table_ref[...].astype(jnp.float32).T.astype(jnp.bfloat16)
    table_t[:, NF:] = jnp.ones((table_t.shape[0], EXTRA), jnp.bfloat16)
    on = active_ref[...].astype(jnp.float32)
    temperature = fields_ref[0].T
    ft[0] = temperature
    scaled = C2 / temperature
    inv_t[...] = scaled
    ratio[...] = jnp.exp(scaled * (SUB * step_w))
    for i in range(1, 6):
        ft[i] = fields_ref[i].T * on
    basis = lax.broadcasted_iota(jnp.int32, (NB, pixels), 0).astype(jnp.float32)
    centre = 300.0 + 2100.0 * basis / (NB - 1)
    row = lax.broadcasted_iota(jnp.int32, (EXTRA, pixels), 0)

    def one_pair(p, carry):
        for h in range(2):
            z = 2 * p + h
            lanes = pl.ds(h * pixels, pixels)
            u = (ft[0, pl.ds(z, 1), :] - centre) * ((NB - 1) / 2100.0)
            bump = jnp.exp(-(u * u))
            for s in range(NS):
                feature = ft[1 + s, pl.ds(z, 1), :] * bump
                weights[p, s * NB : (s + 1) * NB, lanes] = feature.astype(jnp.bfloat16)
            soot = jnp.broadcast_to(ft[5, pl.ds(z, 1), :], (EXTRA, pixels))
            high = soot.astype(jnp.bfloat16).astype(jnp.float32)
            rest = soot - high
            mid = rest.astype(jnp.bfloat16).astype(jnp.float32)
            low = rest - mid
            piece = jnp.where(row == 0, high, jnp.where(row == 1, mid, jnp.where(row == 2, low, 0.0)))
            weights[p, NF:, lanes] = piece.astype(jnp.bfloat16)
        return carry

    lax.fori_loop(0, cells // 2, one_pair, 0)


def compute_block(block, wave0, step_w, table_t, weights, inv_t, ratio, depth, trans, source):
    pixels = inv_t.shape[1]
    chunks = inv_t.shape[0] // (2 * PAIRS)
    groups = BLOCK // SUB
    first = pl.multiple_of(block * BLOCK, BLOCK)
    lhs_rows = pl.ds(first, BLOCK)
    sub = lax.broadcasted_iota(jnp.int32, (SUB, pixels), 0)
    wave = wave0 + step_w * (sub + first).astype(jnp.float32)

    def multiply(q, buf):
        for p in range(PAIRS):
            buf[p] = jnp.dot(
                table_t[lhs_rows, :],
                weights[(chunks - 1 - q) * PAIRS + p],
                preferred_element_type=jnp.float32,
            )

    def march(q, buf, carry):
        total, behind, acc = (list(c) for c in carry)
        base = (chunks - 1 - q) * (2 * PAIRS)
        for i in reversed(range(2 * PAIRS)):
            p, h = divmod(i, 2)
            grow = jnp.exp(wave * inv_t[pl.ds(base + i, 1), :])
            rate = jnp.broadcast_to(ratio[pl.ds(base + i, 1), :], (SUB, pixels))
            for g in range(groups):
                total[g] = total[g] + buf[p, g * SUB : (g + 1) * SUB, h * pixels : (h + 1) * pixels]
                now = jnp.exp2(total[g] * (-LOG2E))
                acc[g] = acc[g] + (behind[g] - now) * pl.reciprocal(grow - 1.0)
                behind[g] = now
                if g + 1 < groups:
                    grow = grow * rate
        return tuple(total), tuple(behind), tuple(acc)

    def two_chunks(i, carry):
        multiply(2 * i + 1, depth[1])
        carry = march(2 * i, depth[0], carry)
        multiply(jnp.minimum(2 * i + 2, chunks - 1), depth[0])
        return march(2 * i + 1, depth[1], carry)

    multiply(0, depth[0])
    zero = jnp.zeros((SUB, pixels), jnp.float32)
    one = jnp.ones((SUB, pixels), jnp.float32)
    start = ((zero,) * groups, (one,) * groups, (zero,) * groups)
    _, behind, acc = lax.fori_loop(0, chunks // 2, two_chunks, start)
    nominal = math.expm1(C2 * 2300.0 / 2000.0)
    for g in range(groups):
        rows = pl.ds(first + g * SUB, SUB)
        rel = (wave + step_w * (g * SUB)) * (1.0 / 2300.0)
        trans[rows, :] = behind[g]
        source[rows, :] = acc[g] * (rel * rel * rel * nominal)


def kernel(
    n_seg, n_band, width_all,
    fields_ref, table_ref, back_ref, active_ref,
    out_ref, mean_ref,
    table_t, weights, inv_t, ratio, ft, depth0, depth1, trans, source, enter, leave, part, parts,
    send_sem, recv_sem, msend, mrecv,
):
    me = lax.axis_index("seg")
    band = lax.axis_index("band")
    width = table_ref.shape[1]
    blocks = width // BLOCK
    step_w = 300.0 / width_all
    wave0 = 2150.0 + step_w * ((band * width).astype(jnp.float32) + 0.5)

    barrier = pltpu.get_barrier_semaphore()

    @pl.when(me > 0)
    def _():
        pl.semaphore_signal(barrier, inc=1, device_id={"seg": me - 1}, device_id_type=MESH)

    @pl.when(me < n_seg - 1)
    def _():
        pl.semaphore_signal(barrier, inc=1, device_id={"seg": me + 1}, device_id_type=MESH)

    for o in range(1, n_band):
        pl.semaphore_signal(
            barrier, inc=1, device_id={"band": lax.rem(band + o, n_band)}, device_id_type=MESH
        )

    prepare(fields_ref, table_ref, active_ref, table_t, weights, inv_t, ratio, ft, step_w)
    part[...] = jnp.zeros_like(part)

    def hop(b):
        rows = pl.ds(pl.multiple_of(b * BLOCK, BLOCK), BLOCK)
        return pltpu.make_async_remote_copy(
            src_ref=leave.at[rows],
            dst_ref=enter.at[rows],
            send_sem=send_sem.at[b],
            recv_sem=recv_sem.at[b],
            device_id={"seg": lax.rem(me + 1, n_seg)},
            device_id_type=MESH,
        )

    def chain(b, carry):
        @pl.when(me > 0)
        def _():
            hop(b).wait_recv()

        rows = pl.ds(pl.multiple_of(b * BLOCK, BLOCK), BLOCK)
        radiance = trans[rows, :] * enter[rows, :] + source[rows, :]
        leave[rows, :] = radiance

        @pl.when(me < n_seg - 1)
        def _():
            hop(b).start()

        part[...] += jnp.sum(radiance.reshape(BLOCK // SUB, SUB, -1), axis=0)
        return carry

    def one_block(t, carry):
        compute_block(
            t, wave0, step_w, table_t, weights, inv_t, ratio, (depth0, depth1), trans, source
        )

        @pl.when(t == 0)
        def _():
            near = (me > 0).astype(jnp.int32) + (me < n_seg - 1).astype(jnp.int32)
            pl.semaphore_wait(barrier, near + (n_band - 1))

        @pl.when(t >= me)
        def _():
            chain(t - me, 0)

        return carry

    @pl.when(me == 0)
    def _():
        enter[...] = back_ref[...].T

    lax.fori_loop(0, blocks, one_block, 0)
    lax.fori_loop(jnp.maximum(blocks - me, 0), blocks, chain, 0)

    def swap(o):
        return pltpu.make_async_remote_copy(
            src_ref=part,
            dst_ref=parts.at[o - 1],
            send_sem=msend.at[o - 1],
            recv_sem=mrecv.at[o - 1],
            device_id={"band": lax.rem(band + o, n_band)},
            device_id_type=MESH,
        )

    for o in range(1, n_band):
        swap(o).start()
    out_ref[...] = leave[...].T

    @pl.when(me < n_seg - 1)
    def _():
        lax.fori_loop(0, blocks, lambda b, c: (hop(b).wait_send(), c)[1], 0)

    total = part[...]
    for o in range(1, n_band):
        swap(o).wait_recv()
        total = total + parts[o - 1]
    mean_ref[...] = jnp.sum(total, axis=0, keepdims=True) * (1.0 / width_all)
    for o in range(1, n_band):
        swap(o).wait_send()


def per_device(n_seg, n_band, fields, spectral_table, background, active):
    rows, cols, cells = fields.shape[1:]
    pixels = rows * cols
    width = spectral_table.shape[1]
    width_all = width * n_band
    blocks = width // BLOCK
    vmem = pl.BlockSpec(memory_space=pltpu.VMEM)
    f32, bf16 = jnp.float32, jnp.bfloat16
    radiance, mean = pl.pallas_call(
        functools.partial(kernel, n_seg, n_band, width_all),
        out_shape=(
            jax.ShapeDtypeStruct((pixels, width), f32),
            jax.ShapeDtypeStruct((1, pixels), f32),
        ),
        in_specs=[vmem] * 4,
        out_specs=(vmem, vmem),
        scratch_shapes=[
            pltpu.VMEM((width, NF + EXTRA), bf16),
            pltpu.VMEM((cells // 2, NF + EXTRA, 2 * pixels), bf16),
            pltpu.VMEM((cells, pixels), f32),
            pltpu.VMEM((cells, pixels), f32),
            pltpu.VMEM((6, cells, pixels), f32),
            pltpu.VMEM((PAIRS, BLOCK, 2 * pixels), f32),
            pltpu.VMEM((PAIRS, BLOCK, 2 * pixels), f32),
            pltpu.VMEM((width, pixels), f32),
            pltpu.VMEM((width, pixels), f32),
            pltpu.VMEM((width, pixels), f32),
            pltpu.VMEM((width, pixels), f32),
            pltpu.VMEM((SUB, pixels), f32),
            pltpu.VMEM((max(n_band - 1, 1), SUB, pixels), f32),
            pltpu.SemaphoreType.DMA((blocks,)),
            pltpu.SemaphoreType.DMA((blocks,)),
            pltpu.SemaphoreType.DMA((max(n_band - 1, 1),)),
            pltpu.SemaphoreType.DMA((max(n_band - 1, 1),)),
        ],
        compiler_params=pltpu.CompilerParams(collective_id=0, has_side_effects=True),
        name="flame",
    )(
        fields.reshape(6, pixels, cells),
        spectral_table,
        background.reshape(pixels, width),
        active.reshape(1, pixels),
    )
    return radiance.reshape(1, rows, cols, width), mean.reshape(1, rows, cols)


def solution(mesh):
    placed = (
        P(None, ("grp", "tile"), None, "seg"),
        P(None, "band"),
        P(("grp", "tile"), None, "band"),
        P(("grp", "tile"), None),
    )
    return jax.shard_map(
        functools.partial(per_device, mesh.shape["seg"], mesh.shape["band"]),
        mesh=mesh,
        in_specs=placed,
        out_specs=(P("seg", ("grp", "tile"), None, "band"), P("seg", ("grp", "tile"), None)),
        check_vma=False,
    )
```

profile of v0, /device:TPU:29, one launch (start us, length us, event | category | flops | bytes accessed | tf_op | source)
XLA Modules:
  0.0 24.7 jit_solution(8234597999563494090)
XLA Ops:
  0.6 21.9 %flame.1 = (f32[128,256]{1,0:T(8,128)}, f32[1,128]{1,0:T(1,128)}) custom-call(f32[6,128,128]{2,1,0:T(8,128)} %bitcast.4, bf16[128,256]{1,0:T(8,128)(2,1)} %table_ref.1, f32[128,256]{1,0:T(8,128)} %bitcast.6, s32[1,128]{1,0:T(1,128)} %active_ref.1), custom_call_target="tpu_custom_call" | custom-call | tf_op jit(solution)/shard_map/flame/pallas_call | solution.py:230
  22.6 0.0 copy-start
  22.6 1.6 %copy.8 = f32[1,1,128,256]{3,2,1,0:T(8,128)} copy(f32[1,1,128,256]{3,2,1,0:T(8,128)} %bitcast.5) | data formatting | bytes 262144
  24.2 0.0 copy-done
  24.2 0.5 %copy.9 = f32[1,1,128]{2,1,0:T(1,128)} copy(f32[1,1,128]{2,1,0:T(1,128)S(1)} %bitcast.7) | data formatting | bytes 1024
Async XLA Ops:
  22.6 1.6 %copy-start = (f32[1,128]{1,0:T(1,128)S(1)}, f32[1,128]{1,0:T(1,128)}, u32[]{:S(2)}) copy-start(f32[1,128]{1,0:T(1,128)} %get-tuple-element.5) | copy-start | bytes 1540
where the time goes:
time: 24.8 us; the launch traced here: 24.7 us
  Pallas kernels  21.9 us (88%)
  local copies, waits for them, and re-layouts  2.08 us (8%)
  between operations  0.65 us (3%)
    pallas_call x1, Pallas kernels, per_device(): pl.pallas_call(functools.partial(kernel, n_seg, n_band, width_all), out_s...  21.9 us
    unnamed x4, local copies, waits for them, and re-layouts  2.08 us

commit v1 on v0

--- a/solution.py
+++ b/solution.py
@@ -16,7 +16,8 @@
 LOG2E = math.log2(math.e)
 SUB = 8
 BLOCK = 64
-PAIRS = 4
+PAIRS = 8
+HOP = 16
 MESH = pl.DeviceIdType.MESH
 
 
@@ -28,9 +29,9 @@
     on = active_ref[...].astype(jnp.float32)
     temperature = fields_ref[0].T
     ft[0] = temperature
-    scaled = C2 / temperature
+    scaled = (C2 * LOG2E) / temperature
     inv_t[...] = scaled
-    ratio[...] = jnp.exp(scaled * (SUB * step_w))
+    ratio[...] = jnp.exp2(scaled * (SUB * step_w))
     for i in range(1, 6):
         ft[i] = fields_ref[i].T * on
     basis = lax.broadcasted_iota(jnp.int32, (NB, pixels), 0).astype(jnp.float32)
@@ -55,7 +56,7 @@
             weights[p, NF:, lanes] = piece.astype(jnp.bfloat16)
         return carry
 
-    lax.fori_loop(0, cells // 2, one_pair, 0)
+    lax.fori_loop(0, cells // 2, one_pair, 0, unroll=4)
 
 
 def compute_block(block, wave0, step_w, table_t, weights, inv_t, ratio, depth, trans, source):
@@ -80,7 +81,7 @@
         base = (chunks - 1 - q) * (2 * PAIRS)
         for i in reversed(range(2 * PAIRS)):
             p, h = divmod(i, 2)
-            grow = jnp.exp(wave * inv_t[pl.ds(base + i, 1), :])
+            grow = jnp.exp2(wave * inv_t[pl.ds(base + i, 1), :])
             rate = jnp.broadcast_to(ratio[pl.ds(base + i, 1), :], (SUB, pixels))
             for g in range(groups):
                 total[g] = total[g] + buf[p, g * SUB : (g + 1) * SUB, h * pixels : (h + 1) * pixels]
@@ -121,6 +122,7 @@
     band = lax.axis_index("band")
     width = table_ref.shape[1]
     blocks = width // BLOCK
+    per = BLOCK // HOP
     step_w = 300.0 / width_all
     wave0 = 2150.0 + step_w * ((band * width).astype(jnp.float32) + 0.5)
 
@@ -142,31 +144,31 @@
     prepare(fields_ref, table_ref, active_ref, table_t, weights, inv_t, ratio, ft, step_w)
     part[...] = jnp.zeros_like(part)
 
-    def hop(b):
-        rows = pl.ds(pl.multiple_of(b * BLOCK, BLOCK), BLOCK)
+    def hop(u):
+        rows = pl.ds(pl.multiple_of(u * HOP, HOP), HOP)
         return pltpu.make_async_remote_copy(
             src_ref=leave.at[rows],
             dst_ref=enter.at[rows],
-            send_sem=send_sem.at[b],
-            recv_sem=recv_sem.at[b],
+            send_sem=send_sem.at[u],
+            recv_sem=recv_sem.at[u],
             device_id={"seg": lax.rem(me + 1, n_seg)},
             device_id_type=MESH,
         )
 
-    def chain(b, carry):
+    def chain(u, carry):
         @pl.when(me > 0)
         def _():
-            hop(b).wait_recv()
-
-        rows = pl.ds(pl.multiple_of(b * BLOCK, BLOCK), BLOCK)
+            hop(u).wait_recv()
+
+        rows = pl.ds(pl.multiple_of(u * HOP, HOP), HOP)
         radiance = trans[rows, :] * enter[rows, :] + source[rows, :]
         leave[rows, :] = radiance
 
         @pl.when(me < n_seg - 1)
         def _():
-            hop(b).start()
-
-        part[...] += jnp.sum(radiance.reshape(BLOCK // SUB, SUB, -1), axis=0)
+            hop(u).start()
+
+        part[...] += jnp.sum(radiance.reshape(HOP // SUB, SUB, -1), axis=0)
         return carry
 
     def one_block(t, carry):
@@ -181,7 +183,7 @@
 
         @pl.when(t >= me)
         def _():
-            chain(t - me, 0)
+            lax.fori_loop((t - me) * per, (t - me + 1) * per, chain, 0)
 
         return carry
 
@@ -190,7 +192,7 @@
         enter[...] = back_ref[...].T
 
     lax.fori_loop(0, blocks, one_block, 0)
-    lax.fori_loop(jnp.maximum(blocks - me, 0), blocks, chain, 0)
+    lax.fori_loop(jnp.maximum(blocks - me, 0) * per, blocks * per, chain, 0)
 
     def swap(o):
         return pltpu.make_async_remote_copy(
@@ -208,7 +210,7 @@
 
     @pl.when(me < n_seg - 1)
     def _():
-        lax.fori_loop(0, blocks, lambda b, c: (hop(b).wait_send(), c)[1], 0)
+        lax.fori_loop(0, blocks * per, lambda u, c: (hop(u).wait_send(), c)[1], 0)
 
     total = part[...]
     for o in range(1, n_band):
@@ -224,7 +226,7 @@
     pixels = rows * cols
     width = spectral_table.shape[1]
     width_all = width * n_band
-    blocks = width // BLOCK
+    hops = width // HOP
     vmem = pl.BlockSpec(memory_space=pltpu.VMEM)
     f32, bf16 = jnp.float32, jnp.bfloat16
     radiance, mean = pl.pallas_call(
@@ -249,12 +251,12 @@
             pltpu.VMEM((width, pixels), f32),
             pltpu.VMEM((SUB, pixels), f32),
             pltpu.VMEM((max(n_band - 1, 1), SUB, pixels), f32),
-            pltpu.SemaphoreType.DMA((blocks,)),
-            pltpu.SemaphoreType.DMA((blocks,)),
+            pltpu.SemaphoreType.DMA((hops,)),
+            pltpu.SemaphoreType.DMA((hops,)),
             pltpu.SemaphoreType.DMA((max(n_band - 1, 1),)),
             pltpu.SemaphoreType.DMA((max(n_band - 1, 1),)),
         ],
-        compiler_params=pltpu.CompilerParams(collective_id=0, has_side_effects=True),
+        compiler_params=pltpu.CompilerParams(collective_id=0, has_side_effects=True, vmem_limit_bytes=24 * 2**20),
         name="flame",
     )(
         fields.reshape(6, pixels, cells),

time: 24.8 us -> 24.2 us (0.976)
  Pallas kernels: 21.9 us -> 18.7 us
  local copies, waits for them, and re-layouts: 2.08 us -> 4.55 us
    pallas_call x1, Pallas kernels: 21.9 us -> 18.7 us  [per_device(): pl.pallas_call(functools.partial(kernel, n_seg, n_band, width_all), out_s...]
    unnamed x4 -> x10, local copies, waits for them, and re-layouts: 2.08 us -> 4.55 us
where the time goes in v1:
time: 24.2 us; the launch traced here: 23.9 us
  Pallas kernels  18.7 us (77%)
  local copies, waits for them, and re-layouts  4.55 us (19%)
  between operations  0.65 us (3%)
    pallas_call x1, Pallas kernels, per_device(): pl.pallas_call(functools.partial(kernel, n_seg, n_band, width_all), out_s...  18.7 us
    unnamed x10, local copies, waits for them, and re-layouts  4.55 us

profile of v1, /device:TPU:29, one launch (start us, length us, event | category | flops | bytes accessed | tf_op | source)
XLA Modules:
  0.0 23.9 jit_solution(15694068725998193478)
XLA Ops:
  0.6 0.0 copy-start.3
  0.6 0.6 %copy-done.3 = s32[1,128]{1,0:T(1,128)S(1)} copy-done((s32[1,128]{1,0:T(1,128)S(1)}, s32[1,128]{1,0:T(1,128)}, u32[]{:S(2)}) %copy-start.3) | copy-done | bytes 536
  1.3 0.0 copy-start
  1.3 1.0 %copy-done = f32[6,1,128,128]{3,2,1,0:T(8,128)S(1)} copy-done((f32[6,1,128,128]{3,2,1,0:T(8,128)S(1)}, f32[6,1,128,128]{3,2,1,0:T(8,128)}, u32[]{:S(2)}) %copy-start) | copy-done | bytes 393240
  2.3 0.0 copy-start.1
  2.3 0.9 %copy-done.1 = f32[1,128,256]{2,1,0:T(8,128)S(1)} copy-done((f32[1,128,256]{2,1,0:T(8,128)S(1)}, f32[1,128,256]{2,1,0:T(8,128)}, u32[]{:S(2)}) %copy-start.1) | copy-done | bytes 131096
  3.2 0.0 copy-start.2
  3.2 0.8 %copy-done.2 = bf16[128,256]{1,0:T(8,128)(2,1)S(1)} copy-done((bf16[128,256]{1,0:T(8,128)(2,1)S(1)}, bf16[128,256]{1,0:T(8,128)(2,1)}, u32[]{:S(2)}) %copy-start.2) | copy-done | bytes 65560
  4.0 18.7 %flame.1 = (f32[128,256]{1,0:T(8,128)S(1)}, f32[1,128]{1,0:T(1,128)S(1)}) custom-call(f32[6,128,128]{2,1,0:T(8,128)S(1)} %bitcast.4, bf16[128,256]{1,0:T(8,128)(2,1)S(1)} %copy-done.2, f32[128,256]{1,0:T(8,128)S(1)} %bitcast.6, s32[1,128]{1,0:T(1,128)S(1)} %copy-done.3), custom_call_target="tpu_custom_call" | custom-call | tf_op jit(solution)/shard_map/flame/pallas_call | solution.py:232
  22.8 0.7 %copy.8 = f32[1,1,128,256]{3,2,1,0:T(8,128)} copy(f32[1,1,128,256]{3,2,1,0:T(8,128)S(1)} %bitcast.5) | data formatting | bytes 262144
  23.4 0.5 %copy.9 = f32[1,1,128]{2,1,0:T(1,128)} copy(f32[1,1,128]{2,1,0:T(1,128)S(1)} %bitcast.7) | data formatting | bytes 1024
Async XLA Ops:
  0.6 0.7 %copy-start.3 = (s32[1,128]{1,0:T(1,128)S(1)}, s32[1,128]{1,0:T(1,128)}, u32[]{:S(2)}) copy-start(s32[1,128]{1,0:T(1,128)} %active_ref.1) | copy-start | bytes 1540
  1.3 1.0 %copy-start = (f32[6,1,128,128]{3,2,1,0:T(8,128)S(1)}, f32[6,1,128,128]{3,2,1,0:T(8,128)}, u32[]{:S(2)}) copy-start(f32[6,1,128,128]{3,2,1,0:T(8,128)} %param.4) | copy-start | bytes 1179652
  2.3 0.9 %copy-start.1 = (f32[1,128,256]{2,1,0:T(8,128)S(1)}, f32[1,128,256]{2,1,0:T(8,128)}, u32[]{:S(2)}) copy-start(f32[1,128,256]{2,1,0:T(8,128)} %param.6) | copy-start | bytes 393220
  3.2 0.8 %copy-start.2 = (bf16[128,256]{1,0:T(8,128)(2,1)S(1)}, bf16[128,256]{1,0:T(8,128)(2,1)}, u32[]{:S(2)}) copy-start(bf16[128,256]{1,0:T(8,128)(2,1)} %table_ref.1) | copy-start | bytes 196612

commit v2 on v1

--- a/solution.py
+++ b/solution.py
@@ -113,11 +113,25 @@
 
 def kernel(
     n_seg, n_band, width_all,
-    fields_ref, table_ref, back_ref, active_ref,
+    fields_hbm, table_hbm, back_hbm, active_hbm,
     out_ref, mean_ref,
     table_t, weights, inv_t, ratio, ft, depth0, depth1, trans, source, enter, leave, part, parts,
+    fields_ref, table_ref, back_ref, active_ref, load_sem,
     send_sem, recv_sem, msend, mrecv,
 ):
+    loads = [
+        pltpu.make_async_copy(src, dst, load_sem.at[i])
+        for i, (src, dst) in enumerate(
+            (
+                (fields_hbm, fields_ref),
+                (active_hbm, active_ref),
+                (table_hbm, table_ref),
+                (back_hbm, back_ref),
+            )
+        )
+    ]
+    for load in loads:
+        load.start()
     me = lax.axis_index("seg")
     band = lax.axis_index("band")
     width = table_ref.shape[1]
@@ -141,6 +155,8 @@
             barrier, inc=1, device_id={"band": lax.rem(band + o, n_band)}, device_id_type=MESH
         )
 
+    for load in loads[:3]:
+        load.wait()
     prepare(fields_ref, table_ref, active_ref, table_t, weights, inv_t, ratio, ft, step_w)
     part[...] = jnp.zeros_like(part)
 
@@ -186,6 +202,8 @@
             lax.fori_loop((t - me) * per, (t - me + 1) * per, chain, 0)
 
         return carry
+
+    loads[3].wait()
 
     @pl.when(me == 0)
     def _():
@@ -235,7 +253,7 @@
             jax.ShapeDtypeStruct((pixels, width), f32),
             jax.ShapeDtypeStruct((1, pixels), f32),
         ),
-        in_specs=[vmem] * 4,
+        in_specs=[pl.BlockSpec(memory_space=pltpu.HBM)] * 4,
         out_specs=(vmem, vmem),
         scratch_shapes=[
             pltpu.VMEM((width, NF + EXTRA), bf16),
@@ -251,6 +269,11 @@
             pltpu.VMEM((width, pixels), f32),
             pltpu.VMEM((SUB, pixels), f32),
             pltpu.VMEM((max(n_band - 1, 1), SUB, pixels), f32),
+            pltpu.VMEM((6, pixels, cells), f32),
+            pltpu.VMEM((NF, width), bf16),
+            pltpu.VMEM((pixels, width), f32),
+            pltpu.VMEM((1, pixels), jnp.int32),
+            pltpu.SemaphoreType.DMA((4,)),
             pltpu.SemaphoreType.DMA((hops,)),
             pltpu.SemaphoreType.DMA((hops,)),
             pltpu.SemaphoreType.DMA((max(n_band - 1, 1),)),
@@ -259,10 +282,10 @@
         compiler_params=pltpu.CompilerParams(collective_id=0, has_side_effects=True, vmem_limit_bytes=24 * 2**20),
         name="flame",
     )(
-        fields.reshape(6, pixels, cells),
-        spectral_table,
-        background.reshape(pixels, width),
-        active.reshape(1, pixels),
+        pltpu.with_memory_space_constraint(fields.reshape(6, pixels, cells), pltpu.HBM),
+        pltpu.with_memory_space_constraint(spectral_table, pltpu.HBM),
+        pltpu.with_memory_space_constraint(background.reshape(pixels, width), pltpu.HBM),
+        pltpu.with_memory_space_constraint(active.reshape(1, pixels), pltpu.HBM),
     )
     return radiance.reshape(1, rows, cols, width), mean.reshape(1, rows, cols)
 

time: 24.2 us -> 21.8 us (0.901)
  local copies, waits for them, and re-layouts: 4.55 us -> 1.17 us
  Pallas kernels: 18.7 us -> 19.8 us
    unnamed x10 -> x2, local copies, waits for them, and re-layouts: 4.55 us -> 1.17 us
    pallas_call x1, Pallas kernels: 18.7 us -> 19.8 us  [per_device(): pl.pallas_call(functools.partial(kernel, n_seg, n_band, width_all), out_s...]
where the time goes in v2:
time: 21.8 us; the launch traced here: 21.6 us
  Pallas kernels  19.8 us (91%)
  local copies, waits for them, and re-layouts  1.17 us (5%)
  between operations  0.64 us (3%)
    pallas_call x1, Pallas kernels, per_device(): pl.pallas_call(functools.partial(kernel, n_seg, n_band, width_all), out_s...  19.8 us
    unnamed x2, local copies, waits for them, and re-layouts  1.17 us

profile of v2, /device:TPU:29, one launch (start us, length us, event | category | flops | bytes accessed | tf_op | source)
XLA Modules:
  0.0 21.6 jit_solution(1847019056553148551)
XLA Ops:
  0.6 19.8 %flame.1 = (f32[128,256]{1,0:T(8,128)S(1)}, f32[1,128]{1,0:T(1,128)S(1)}) custom-call(f32[6,128,128]{2,1,0:T(8,128)} %bitcast.6, bf16[128,256]{1,0:T(8,128)(2,1)} %table_hbm.1, f32[128,256]{1,0:T(8,128)} %bitcast.7, s32[1,128]{1,0:T(1,128)} %active_hbm.1), custom_call_target="tpu_custom_call" | custom-call | tf_op jit(solution)/shard_map/flame/pallas_call | solution.py:250
  20.5 0.7 %copy.8 = f32[1,1,128,256]{3,2,1,0:T(8,128)} copy(f32[1,1,128,256]{3,2,1,0:T(8,128)S(1)} %bitcast.4) | data formatting | bytes 262144
  21.1 0.5 %copy.9 = f32[1,1,128]{2,1,0:T(1,128)} copy(f32[1,1,128]{2,1,0:T(1,128)S(1)} %bitcast.5) | data formatting | bytes 1024
